TPU v7x, 32 devices: a whole 2x2x4 slice. The times are simulated.
32 devices in a mesh: val: 8 (over y, x, core), cond: 4 (over z).
Axes of the slice: x: 2, y: 2, z: 4, core: 2. Of those that a mesh axis runs over, the one named last changes fastest.
Arguments:
- trial: bfloat16 [256, 65536], P('val', 'cond'), may hold values from -6 to 6
- pair_cond: bfloat16 [80, 1024, 1024], P('val', 'cond'), may hold values from -0.1875 to 0.1875
- pair_val: bfloat16 [256, 20480], P(None, 'val'), may hold values from -0.0625 to 0.0625
Outputs:
- applied: bfloat16 [256, 65536], P('val', 'cond')
All inputs are finite; a program needn't handle non-finite values.
Results may differ from a plain program's by a relative error of at most 0.0049.
Values may be sent and summed in bfloat16 or wider, within the bound.
No kernel may reach another device: no remote copies, remote signals or barrier semaphores. Data moves between devices by JAX's collectives and lax.ppermute only.
A program may use at most 320 MiB of HBM per device.

v0:
```python
import jax
import jax.numpy as jnp
from jax import lax
from jax.experimental import pallas as pl
from jax.experimental.pallas import tpu as pltpu
from jax.sharding import PartitionSpec as P


S = 64
CHUNKS = 4
GROUPS = 1

NT = (((1,), (1,)), ((), ()))
NN = (((1,), (0,)), ((), ()))


def group_size(count, rows):
    best = 1
    for size in range(1, count + 1):
        if count % size == 0 and size * rows <= 256:
            best = size
    return best


def chain(zed, entries, pc, accs):
    pieces, count, rows, depth = entries[0][0][0].shape
    total_g, cols, _ = pc.shape
    bands = entries[0][0][1].shape[2]
    many = len(entries[0])
    gg = group_size(total_g, rows * many)
    step_g = gg * GROUPS if total_g % (gg * GROUPS) == 0 else gg
    high = gg * many * rows
    first = [acc is None for acc in accs]

    def kernel(zed_ref, *refs):
        refs = list(refs)
        pc_ref = refs.pop(0)
        zed_at = zed_ref[0]
        t_refs = [[refs.pop(0) for _ in entry] for entry in entries]
        pv_refs = [[refs.pop(0) for _ in entry] for entry in entries]
        acc_refs = [None if f else refs.pop(0) for f in first]
        out_refs = [refs.pop(0) for _ in entries]
        token_ref, inner_ref = refs

        @pl.when(pl.program_id(0) == 0)
        def _():
            token_ref[...] = jnp.zeros(token_ref.shape, jnp.float32)
            for acc_ref, out_ref in zip(acc_refs, out_refs):
                if acc_ref is None:
                    out_ref[...] = jnp.zeros(out_ref.shape, jnp.float32)
                else:
                    out_ref[...] = acc_ref[...]

        for e in range(len(entries)):
            for base in range(0, step_g, gg):
                stacked = jnp.concatenate(
                    [pv_refs[e][u][base + g] for g in range(gg) for u in range(many)], axis=0)
                left = stacked.T
                for g in range(gg):
                    for u in range(many):
                        low = (g * many + u) * rows
                        inner = None
                        for d in range(pieces):
                            q = lax.rem(zed_at + (pieces - d), pieces)
                            if depth % 128:
                                weights = pc_ref[d, base + g]
                            else:
                                weights = pc_ref[base + g, :, d * depth:(d + 1) * depth]
                            part = lax.dot_general(
                                t_refs[e][u][q].reshape(count * rows, depth), weights, NT,
                                preferred_element_type=jnp.float32)
                            inner = part if inner is None else inner + part
                        inner_ref[e, :, low:low + rows, :] = inner.astype(jnp.bfloat16).reshape(count, rows, cols)
                for s in range(count):
                    out_refs[e][s] += lax.dot_general(left, inner_ref[e, s], NN, preferred_element_type=jnp.float32)

    def fixed(i, z):
        return (0, 0, 0)

    if depth % 128:
        pc = pc.reshape(total_g, cols, pieces, depth).transpose(2, 0, 1, 3)
        in_specs = [pl.BlockSpec((pieces, step_g, cols, depth), lambda i, z: (0, i, 0, 0))]
    else:
        in_specs = [pl.BlockSpec((step_g, cols, pieces * depth), lambda i, z: (i, 0, 0))]
    flat = [unit for entry in entries for unit in entry]
    in_specs += [pl.BlockSpec((pieces, count, rows, depth), lambda i, z: (0, 0, 0, 0)) for _ in flat]
    in_specs += [pl.BlockSpec((step_g, rows, bands), lambda i, z: (i, 0, 0)) for _ in flat]
    operands = [pc] + [t for t, _ in flat] + [pv for _, pv in flat]
    aliases = {}
    for e, acc in enumerate(accs):
        if acc is not None:
            in_specs.append(pl.BlockSpec((count, bands, cols), fixed))
            operands.append(acc)
            aliases[len(operands)] = e
    flops = 2 * len(flat) * count * total_g * rows * cols * (pieces * depth + bands)
    *outs, token = pl.pallas_call(
        kernel,
        out_shape=[jax.ShapeDtypeStruct((count, bands, cols), jnp.float32) for _ in entries]
        + [jax.ShapeDtypeStruct((8, 128), jnp.float32)],
        grid_spec=pltpu.PrefetchScalarGridSpec(
            num_scalar_prefetch=1,
            grid=(total_g // step_g,),
            in_specs=in_specs,
            out_specs=[pl.BlockSpec((count, bands, cols), fixed) for _ in entries]
            + [pl.BlockSpec((8, 128), lambda i, z: (0, 0))],
            scratch_shapes=[pltpu.VMEM((len(entries), count, high, cols), jnp.bfloat16)],
        ),
        input_output_aliases=aliases,
        compiler_params=pltpu.CompilerParams(
            dimension_semantics=("arbitrary",), vmem_limit_bytes=56 * 1024 * 1024),
        cost_estimate=pl.CostEstimate(
            flops=flops, transcendentals=0,
            bytes_accessed=total_g * cols * depth * pieces * 2 + len(entries) * count * bands * cols * 8),
        name="chain",
    )(zed, *operands)
    return outs, token


def after(value, *tokens):
    return lax.optimization_barrier((value, *tokens))[0]


def make_body(mesh):
    nv, nc = mesh.shape["val"], mesh.shape["cond"]
    nx = nv // 4

    def split(i):
        return i // (2 * nx), (i // 2) % nx, i % 2

    def join(y, x, k):
        return (y * nx + x) * 2 + k

    def flip_y(i):
        return lax.rem(i + 2 * nx, nv) if not isinstance(i, int) else (i + 2 * nx) % nv

    def send(value, table):
        return lax.ppermute(value, "val", table)

    to_twin = [(i, i ^ 1) for i in range(nv)]
    to_y = [(i, (i + 2 * nx) % nv) for i in range(nv)]

    def to_x(step):
        return [(i, join(split(i)[0], (split(i)[1] + step) % nx, split(i)[2])) for i in range(nv)]

    def to_z(step):
        return [(j, (j + step) % nc) for j in range(nc)]

    def body(trial, pair_cond, pair_val):
        me = lax.axis_index("val")
        zed = lax.axis_index("cond").astype(jnp.int32).reshape(1)
        core = lax.rem(me, 2)
        own_x = lax.rem(me // 2, nx)
        own_y = me // (2 * nx)
        wb = trial.shape[0]
        depth = trial.shape[1] // S
        bands = pair_val.shape[0]
        gb, cols, _ = pair_cond.shape
        vb = bands // nv
        half = S // 2
        n = half // CHUNKS

        pc_y = send(pair_cond, to_y)

        turned = trial.reshape(wb, depth, S).transpose(2, 0, 1)
        kept = lax.dynamic_slice_in_dim(turned, core * half, half, 0)
        given = lax.dynamic_slice_in_dim(turned, (1 - core) * half, half, 0)
        taken = send(given, to_twin)
        block = jnp.concatenate([kept, taken], axis=1)

        def around_z(part):
            return [part] + [lax.ppermute(part, "cond", to_z(q)) for q in range(1, nc)]

        parts = [around_z(block[:n])]

        flat = after(pair_val, block).T.reshape(wb, nv, gb, bands).transpose(1, 2, 0, 3)

        def blocks_for(dest):
            order = (dest, dest ^ 1, flip_y(dest), flip_y(dest) ^ 1)
            return jnp.stack([lax.dynamic_index_in_dim(flat, o, 0, keepdims=False) for o in order])

        def swap_pairs(a):
            return jnp.stack([a[1], a[0], a[3], a[2]])

        mine, twins = blocks_for(me), blocks_for(me ^ 1)
        far = []
        for step in range(1, nx):
            dest = (own_y * nx + lax.rem(own_x + step, nx)) * 2 + core
            far.append(blocks_for(dest))
        pv_near = jnp.concatenate([mine, send(twins, to_twin)], axis=2)
        far_got = [send(f, to_x(step)) for f, step in zip(far, range(1, nx))]
        pc_own = jnp.concatenate([pair_cond, send(after(pair_cond, block), to_twin)], axis=0)
        for i in range(1, CHUNKS):
            parts.append(around_z(after(block[i * n:(i + 1) * n], *far)))

        def own_pv(pv):
            return pv[:2].reshape(2 * gb, 2 * wb, bands)

        accs = [None] * CHUNKS
        near, others = [None] * CHUNKS, [None] * CHUNKS
        token = None
        pv_all = [pv_near]
        for i in range(CHUNKS):
            got = list(lax.optimization_barrier((*parts[i], pc_own if token is None else token))[:-1])
            near[i] = jnp.stack(got)
            others[i] = [send(near[i], to_x(step)) for step in range(1, nx)]
            work = [(i, [(near[i], own_pv(pv_near))])]
            if i:
                for u in range(1, nx):
                    other = after(others[i - 1][u - 1], token)
                    work.append((i - 1, [(other, own_pv(pv_all[u]))]))
            for w in (work if nx > 2 else [work]):
                w = w if isinstance(w, list) else [w]
                outs, token = chain(zed, [e for _, e in w], pc_own, [accs[j] for j, _ in w])
                for (j, _), out in zip(w, outs):
                    accs[j] = out
            if i == 0:
                for got in far_got:
                    got = after(got, token)
                    pv_all.append(jnp.concatenate([got, send(swap_pairs(got), to_twin)], axis=2))
        pc_y = after(pc_y, token)
        pc_yt = send(pc_y, to_twin)

        def both(i, u, which):
            return [(t, pv[2 + which]) for t, pv in list(zip([near[i]] + others[i], pv_all))[u:u + 2]]

        def far_call(chunks, which, pc, token):
            for u in range(0, nx, 2):
                outs, token = chain(
                    zed, [both(i, u, which) for i in chunks], after(pc, token), [accs[i] for i in chunks])
                for i, out in zip(chunks, outs):
                    accs[i] = out
            return token

        last = CHUNKS - 1
        token = far_call([0, 1], 0, pc_y, token)
        for u in range(1, nx):
            (accs[last],), token = chain(
                zed, [[(after(others[last][u - 1], token), own_pv(pv_all[u]))]], pc_own, [accs[last]])
        token = far_call([2, 3], 0, pc_y, token)

        def reduced(i):
            shaped = accs[i].reshape(n, 2, nx, 2 * vb, cols)

            def rows_of(y, x):
                block = lax.dynamic_slice(shaped, (0, y, x, 0, 0), (n, 1, 1, 2 * vb, cols))
                return block.reshape(n, 2 * vb, cols)

            total = rows_of(own_y, own_x)
            for dy in range(2):
                for dx in range(nx):
                    if dy or dx:
                        x = lax.rem(own_x + dx, nx)
                        y = own_y if dy == 0 else 1 - own_y
                        table = [
                            (j, join((split(j)[0] + dy) % 2, (split(j)[1] + dx) % nx, split(j)[2])) for j in range(nv)]
                        total = total + send(rows_of(y, x).astype(jnp.bfloat16), table).astype(jnp.float32)
            return total.astype(jnp.bfloat16)

        finals = []
        for chunks in ([0, 1], [2], [3]):
            token = far_call(chunks, 1, pc_yt, token)
            finals += [reduced(i) for i in chunks]
        done = jnp.concatenate(finals, axis=0).reshape(half, 2, vb, cols)
        mine = lax.dynamic_index_in_dim(done, core, 1, keepdims=False)
        other = send(lax.dynamic_index_in_dim(done, 1 - core, 1, keepdims=False), to_twin)
        low = jnp.where(core == 0, mine, other)
        high = jnp.where(core == 0, other, mine)
        whole = jnp.concatenate([low, high], axis=0)
        return whole.transpose(1, 2, 0).reshape(vb, cols * S)

    return body


def solution(mesh):
    placed = (P("val", "cond"), P("val", "cond", None), P(None, "val"))
    body = make_body(mesh)

    return jax.shard_map(body, mesh=mesh, in_specs=placed, out_specs=P("val", "cond"), check_vma=False)
```

profile of v0, /device:TPU:0, one launch (start us, length us, event | category | flops | bytes accessed | tf_op | source)
XLA Modules:
  0.0 335.5 jit_solution(6411831682647259604)
XLA Ops:
  0.0 3.0 reshape.76
  3.0 3.3 constant_dynamic-slice_fusion.12
  13.9 5.5 %constant_dynamic-update-slice_fusion.1 = bf16[20,256,1024]{2,1,0:T(8,128)(2,1)} fusion(bf16[10,256,1024]{2,1,0:T(8,128)(2,1)} %param.4), kind=kLoop, calls=%fused_computation.82 | loop fusion | bytes 10485760
  21.5 3.6 %collective-permute-start.14 = (bf16[8,64,256]{2,1,0:T(8,128)(2,1)}, bf16[8,64,256]{2,1,0:T(8,128)(2,1)}, u32[]{:S(2)}, u32[]{:S(2)}) collective-permute-start(bf16[8,64,256]{2,1,0:T(8,128)(2,1)} %get-tuple-element.57), channel_id=1, source_target_pairs={{0,3},{1,0},{2,1},{3,2},{4,7},{5,4},{6,5},{7,6},{8,11},{9,8},{10,9... | collective-permute-start | bytes 786440 | tf_op jit(solution)/shard_map/ppermute | solution.py:171
  32.6 5.5 %constant_dynamic-update-slice_fusion.refs_0_ = bf16[20,256,1024]{2,1,0:T(8,128)(2,1)} fusion(bf16[20,256,1024]{2,1,0:T(8,128)(2,1)} %constant_dynamic-update-slice_fusion.1, bf16[10,256,1024]{2,1,0:T(8,128)(2,1)} %collective-permute-done.2), kind=kLoop, calls=%fused_computation.81 | loop fusion | bytes 10485760 | tf_op jit(solution)/shard_map/concatenate | solution.py:191
  38.0 2.8 collective-permute-start.11
  40.8 8.1 %collective-permute-done.13 = bf16[8,64,256]{2,1,0:T(8,128)(2,1)} collective-permute-done((bf16[8,64,256]{2,1,0:T(8,128)(2,1)}, bf16[8,64,256]{2,1,0:T(8,128)(2,1)}, u32[]{:S(2)}, u32[]{:S(2)}) %collective-permute-start.13) | collective-permute-done | bytes 262176 | tf_op jit(solution)/shard_map/ppermute | solution.py:171
  51.7 11.5 %chain.10 = (f32[8,256,256]{2,1,0:T(8,128)}, f32[8,128]{1,0:T(8,128)}) custom-call(s32[1]{0:T(128)} %bitcast.zed_ref, bf16[20,256,1024]{2,1,0:T(8,128)(2,1)} %constant_dynamic-update-slice_fusion.refs_0_, bf16[4,8,64,256]{3,2,1,0:T(8,128)(2,1)} %copy-done.2, bf16[20,64,256]{2,1,0:T(8,128)(2,1)} %bitcast.186), custom_call_target="tpu_custom_call" | custom-call | flops 6710886400 | bytes 14680064 | tf_op jit(solution)/shard_map/chain/pallas_call | solution.py:96
  63.4 7.4 %collective-permute-start.10 = (bf16[8,64,256]{2,1,0:T(8,128)(2,1)S(1)}, bf16[8,64,256]{2,1,0:T(8,128)(2,1)S(1)}, u32[]{:S(2)}, u32[]{:S(2)}) collective-permute-start(bf16[8,64,256]{2,1,0:T(8,128)(2,1)S(1)} %copy-done.7), channel_id=1, source_target_pairs={{0,2},{1,3},{2,0},{3,1},{4,6},{5,7},{6,4},{7,5},{8,10},{9,11},{10,... | collective-permute-start | bytes 786440 | tf_op jit(solution)/shard_map/ppermute | solution.py:171
  70.8 18.1 %collective-permute-done.10 = bf16[8,64,256]{2,1,0:T(8,128)(2,1)S(1)} collective-permute-done((bf16[8,64,256]{2,1,0:T(8,128)(2,1)S(1)}, bf16[8,64,256]{2,1,0:T(8,128)(2,1)S(1)}, u32[]{:S(2)}, u32[]{:S(2)}) %collective-permute-start.10) | collective-permute-done | bytes 262176 | tf_op jit(solution)/shard_map/ppermute | solution.py:171
  93.3 19.8 %chain.11 = (f32[8,256,256]{2,1,0:T(8,128)}, f32[8,256,256]{2,1,0:T(8,128)}, f32[8,128]{1,0:T(8,128)}) custom-call(s32[1]{0:T(128)} %bitcast.zed_ref, bf16[20,256,1024]{2,1,0:T(8,128)(2,1)} %constant_dynamic-update-slice_fusion.refs_0_, bf16[4,8,64,256]{3,2,1,0:T(8,128)(2,1)} %copy-done.3, ...), custom_call_target="tpu_custom_call", output_to_operand_aliasing={{1}: (6, {})} | custom-call | flops 13421772800 | bytes 18874368 | tf_op jit(solution)/shard_map/chain/pallas_call | solution.py:96
  113.1 3.6 %collective-permute-done.19.refs_2_.refs_4_ = bf16[4,8,64,256]{3,2,1,0:T(8,128)(2,1)S(1)} collective-permute-done((bf16[4,8,64,256]{3,2,1,0:T(8,128)(2,1)S(1)}, bf16[4,8,64,256]{3,2,1,0:T(8,128)(2,1)S(1)}, u32[]{:S(2)}, u32[]{:S(2)}) %collective-permute-start.19) | collective-permute-done | bytes 1048608 | tf_op jit(solution)/shard_map/ppermute | solution.py:137
  122.6 19.7 %chain.12 = (f32[8,256,256]{2,1,0:T(8,128)}, f32[8,256,256]{2,1,0:T(8,128)}, f32[8,128]{1,0:T(8,128)}) custom-call(s32[1]{0:T(128)} %bitcast.zed_ref, bf16[20,256,1024]{2,1,0:T(8,128)(2,1)} %constant_dynamic-update-slice_fusion.refs_0_, bf16[4,8,64,256]{3,2,1,0:T(8,128)(2,1)} %copy-done.4, ...), custom_call_target="tpu_custom_call", output_to_operand_aliasing={{1}: (6, {})} | custom-call | flops 13421772800 | bytes 18874368 | tf_op jit(solution)/shard_map/chain/pallas_call | solution.py:96
  145.1 19.7 %chain.13 = (f32[8,256,256]{2,1,0:T(8,128)}, f32[8,256,256]{2,1,0:T(8,128)}, f32[8,128]{1,0:T(8,128)}) custom-call(s32[1]{0:T(128)} %bitcast.zed_ref, bf16[20,256,1024]{2,1,0:T(8,128)(2,1)} %constant_dynamic-update-slice_fusion.refs_0_, bf16[4,8,64,256]{3,2,1,0:T(8,128)(2,1)} %pad_maximum_fusion.5.refs_1_.refs_3_, ...), custom_call_target="tpu_custom_call", output_to_operand_aliasing={{1}: (6, {})} | custom-call | flops 13421772800 | bytes 18874368 | tf_op jit(solution)/shard_map/chain/pallas_call | solution.py:96
  167.7 23.1 %collective-permute-done.28.refs_1_.refs_4_.refs_2_ = bf16[4,8,64,256]{3,2,1,0:T(8,128)(2,1)} collective-permute-done((bf16[4,8,64,256]{3,2,1,0:T(8,128)(2,1)}, bf16[4,8,64,256]{3,2,1,0:T(8,128)(2,1)}, u32[]{:S(2)}, u32[]{:S(2)}) %collective-permute-start.28) | collective-permute-done | bytes 1048608 | tf_op jit(solution)/shard_map/ppermute | solution.py:137
  190.8 12.1 %chain.16 = (f32[8,256,256]{2,1,0:T(8,128)}, f32[8,128]{1,0:T(8,128)}) custom-call(s32[1]{0:T(128)} %bitcast.zed_ref, bf16[20,256,1024]{2,1,0:T(8,128)(2,1)} %constant_dynamic-update-slice_fusion.refs_0_, bf16[4,8,64,256]{3,2,1,0:T(8,128)(2,1)} %collective-permute-done.28.refs_1_.refs_4_.refs_2_, ...), custom_call_target="tpu_custom_call", output_to_operand_aliasing={{0}: (4, {})} | custom-call | flops 6710886400 | bytes 14680064 | tf_op jit(solution)/shard_map/chain/pallas_call | solution.py:96
  202.9 20.7 %chain.14 = (f32[8,256,256]{2,1,0:T(8,128)}, f32[8,256,256]{2,1,0:T(8,128)}, f32[8,128]{1,0:T(8,128)}) custom-call(s32[1]{0:T(128)} %bitcast.zed_ref, bf16[10,256,1024]{2,1,0:T(8,128)(2,1)} %collective-permute-done.refs_0_, bf16[4,8,64,256]{3,2,1,0:T(8,128)(2,1)} %copy-done.2, ...), custom_call_target="tpu_custom_call", output_to_operand_aliasing={{0}: (10, {}), {1}: (11, {})} | custom-call | flops 13421772800 | bytes 13631488 | tf_op jit(solution)/shard_map/chain/pallas_call | solution.py:96
  223.6 20.7 %chain.17 = (f32[8,256,256]{2,1,0:T(8,128)}, f32[8,256,256]{2,1,0:T(8,128)}, f32[8,128]{1,0:T(8,128)}) custom-call(s32[1]{0:T(128)} %bitcast.zed_ref, bf16[10,256,1024]{2,1,0:T(8,128)(2,1)} %collective-permute-done.refs_0_, bf16[4,8,64,256]{3,2,1,0:T(8,128)(2,1)} %copy-done.4, ...), custom_call_target="tpu_custom_call", output_to_operand_aliasing={{0}: (10, {}), {1}: (11, {})} | custom-call | flops 13421772800 | bytes 13631488 | tf_op jit(solution)/shard_map/chain/pallas_call | solution.py:96
  244.4 20.9 %chain.15 = (f32[8,256,256]{2,1,0:T(8,128)}, f32[8,256,256]{2,1,0:T(8,128)}, f32[8,128]{1,0:T(8,128)}) custom-call(s32[1]{0:T(128)} %bitcast.zed_ref, bf16[10,256,1024]{2,1,0:T(8,128)(2,1)} %collective-permute-done.21.refs_0_, bf16[4,8,64,256]{3,2,1,0:T(8,128)(2,1)} %copy-done.2, ...), custom_call_target="tpu_custom_call", output_to_operand_aliasing={{0}: (10, {}), {1}: (11, {})} | custom-call | flops 13421772800 | bytes 13631488 | tf_op jit(solution)/shard_map/chain/pallas_call | solution.py:96
  273.3 12.2 %chain.19 = (f32[8,256,256]{2,1,0:T(8,128)}, f32[8,128]{1,0:T(8,128)}) custom-call(s32[1]{0:T(128)} %bitcast.zed_ref, bf16[10,256,1024]{2,1,0:T(8,128)(2,1)} %collective-permute-done.21.refs_0_, bf16[4,8,64,256]{3,2,1,0:T(8,128)(2,1)} %pad_maximum_fusion.5.refs_1_.refs_3_, ...), custom_call_target="tpu_custom_call", output_to_operand_aliasing={{0}: (6, {})} | custom-call | flops 6710886400 | bytes 9437184 | tf_op jit(solution)/shard_map/chain/pallas_call | solution.py:96
  285.5 12.3 %chain.18 = (f32[8,256,256]{2,1,0:T(8,128)}, f32[8,128]{1,0:T(8,128)}) custom-call(s32[1]{0:T(128)} %bitcast.zed_ref, bf16[10,256,1024]{2,1,0:T(8,128)(2,1)} %collective-permute-done.21.refs_0_, bf16[4,8,64,256]{3,2,1,0:T(8,128)(2,1)} %copy-done.4, bf16[4,8,64,256]{3,2,1,0:T(8,128)(2,1)} %copy-done.9, ...), custom_call_target="tpu_custom_call", output_to_operand_aliasing={{0}: (6, {})} | custom-call | flops 6710886400 | bytes 9437184 | tf_op jit(solution)/shard_map/chain/pallas_call | solution.py:96
  311.4 3.6 %collective-permute-done.29 = bf16[8,64,256]{2,1,0:T(8,128)(2,1)S(1)} collective-permute-done((bf16[8,64,256]{2,1,0:T(8,128)(2,1)S(1)}, bf16[8,64,256]{2,1,0:T(8,128)(2,1)S(1)}, u32[]{:S(2)}, u32[]{:S(2)}) %collective-permute-start.29) | collective-permute-done | bytes 262176 | tf_op jit(solution)/shard_map/ppermute | solution.py:137
  317.2 3.4 %collective-permute-done.31 = bf16[8,64,256]{2,1,0:T(8,128)(2,1)S(1)} collective-permute-done((bf16[8,64,256]{2,1,0:T(8,128)(2,1)S(1)}, bf16[8,64,256]{2,1,0:T(8,128)(2,1)S(1)}, u32[]{:S(2)}, u32[]{:S(2)}) %collective-permute-start.31) | collective-permute-done | bytes 262176 | tf_op jit(solution)/shard_map/ppermute | solution.py:137
  321.8 4.5 %collective-permute-done.32 = bf16[8,64,256]{2,1,0:T(8,128)(2,1)S(1)} collective-permute-done((bf16[8,64,256]{2,1,0:T(8,128)(2,1)S(1)}, bf16[8,64,256]{2,1,0:T(8,128)(2,1)S(1)}, u32[]{:S(2)}, u32[]{:S(2)}) %collective-permute-start.32) | collective-permute-done | bytes 262176 | tf_op jit(solution)/shard_map/ppermute | solution.py:137
  (125 shorter events, 70.0 us)
Async XLA Ops:
  10.8 20.2 %collective-permute-start.2 = (bf16[10,256,1024]{2,1,0:T(8,128)(2,1)}, bf16[10,256,1024]{2,1,0:T(8,128)(2,1)}, u32[]{:S(2)}, u32[]{:S(2)}) collective-permute-start(bf16[10,256,1024]{2,1,0:T(8,128)(2,1)} %param.4), channel_id=1, source_target_pairs={{0,4},{4,0},{8,12},{12,8},{16,20},{20,16},{24,28},{28,24},{1,5},{5... | collective-permute-start | bytes 15728648 | tf_op jit(solution)/shard_map/ppermute | solution.py:137
  11.2 153.6 %collective-permute-start = (bf16[10,256,1024]{2,1,0:T(8,128)(2,1)}, bf16[10,256,1024]{2,1,0:T(8,128)(2,1)}, u32[]{:S(2)}, u32[]{:S(2)}) collective-permute-start(bf16[10,256,1024]{2,1,0:T(8,128)(2,1)} %param.4), channel_id=1, source_target_pairs={{0,16},{4,20},{8,24},{12,28},{16,0},{20,4},{24,8},{28,12},{1,17},{... | collective-permute-start | bytes 15728648 | tf_op jit(solution)/shard_map/ppermute | solution.py:137
  25.1 23.8 %collective-permute-start.13 = (bf16[8,64,256]{2,1,0:T(8,128)(2,1)}, bf16[8,64,256]{2,1,0:T(8,128)(2,1)}, u32[]{:S(2)}, u32[]{:S(2)}) collective-permute-start(bf16[8,64,256]{2,1,0:T(8,128)(2,1)} %get-tuple-element.57), channel_id=1, source_target_pairs={{0,2},{1,3},{2,0},{3,1},{4,6},{5,7},{6,4},{7,5},{8,10},{9,11},{10,... | collective-permute-start | bytes 786440 | tf_op jit(solution)/shard_map/ppermute | solution.py:171
  31.1 32.1 %collective-permute-start.17 = (bf16[4,10,32,256]{3,2,1,0:T(8,128)(2,1)S(1)}, bf16[4,10,32,256]{3,2,1,0:T(8,128)(2,1)S(1)}, u32[]{:S(2)}, u32[]{:S(2)}) collective-permute-start(bf16[4,10,32,256]{3,2,1,0:T(8,128)(2,1)S(1)} %pad_maximum_fusion.7), channel_id=1, source_target_pairs={{0,8},{4,12},{8,0},{12,4},{16,24},{20,28},{24,16},{28,20},{1,9},{5... | collective-permute-start | bytes 1966088 | tf_op jit(solution)/shard_map/ppermute | solution.py:137
  38.0 32.8 %collective-permute-start.11 = (bf16[8,64,256]{2,1,0:T(8,128)(2,1)S(1)}, bf16[8,64,256]{2,1,0:T(8,128)(2,1)S(1)}, u32[]{:S(2)}, u32[]{:S(2)}) collective-permute-start(bf16[8,64,256]{2,1,0:T(8,128)(2,1)S(1)} %copy-done.7), channel_id=1, source_target_pairs={{0,3},{1,0},{2,1},{3,2},{4,7},{5,4},{6,5},{7,6},{8,11},{9,8},{10,9... | collective-permute-start | bytes 786440 | tf_op jit(solution)/shard_map/ppermute | solution.py:171
  50.2 42.3 %collective-permute-start.16 = (bf16[4,8,64,256]{3,2,1,0:T(8,128)(2,1)S(1)}, bf16[4,8,64,256]{3,2,1,0:T(8,128)(2,1)}, u32[]{:S(2)}, u32[]{:S(2)}) collective-permute-start(bf16[4,8,64,256]{3,2,1,0:T(8,128)(2,1)S(1)} %pad_maximum_fusion.2.refs_1_), channel_id=1, source_target_pairs={{0,8},{4,12},{8,0},{12,4},{16,24},{20,28},{24,16},{28,20},{1,9},{5... | collective-permute-start | bytes 3145736 | tf_op jit(solution)/shard_map/ppermute | solution.py:137
  63.3 25.9 %collective-permute-start.18 = (bf16[4,10,32,256]{3,2,1,0:T(8,128)(2,1)S(1)}, bf16[4,10,32,256]{3,2,1,0:T(8,128)(2,1)S(1)}, u32[]{:S(2)}, u32[]{:S(2)}) collective-permute-start(bf16[4,10,32,256]{3,2,1,0:T(8,128)(2,1)S(1)} %pad_maximum_fusion.9), channel_id=1, source_target_pairs={{0,4},{4,0},{8,12},{12,8},{16,20},{20,16},{24,28},{28,24},{1,5},{5... | collective-permute-start | bytes 1966088 | tf_op jit(solution)/shard_map/ppermute | solution.py:137
  63.4 25.6 %collective-permute-start.10 = (bf16[8,64,256]{2,1,0:T(8,128)(2,1)S(1)}, bf16[8,64,256]{2,1,0:T(8,128)(2,1)S(1)}, u32[]{:S(2)}, u32[]{:S(2)}) collective-permute-start(bf16[8,64,256]{2,1,0:T(8,128)(2,1)S(1)} %copy-done.7), channel_id=1, source_target_pairs={{0,2},{1,3},{2,0},{3,1},{4,6},{5,7},{6,4},{7,5},{8,10},{9,11},{10,... | collective-permute-start | bytes 786440 | tf_op jit(solution)/shard_map/ppermute | solution.py:171
  89.0 30.2 %collective-permute-start.8 = (bf16[8,64,256]{2,1,0:T(8,128)(2,1)S(1)}, bf16[8,64,256]{2,1,0:T(8,128)(2,1)S(1)}, u32[]{:S(2)}, u32[]{:S(2)}) collective-permute-start(bf16[8,64,256]{2,1,0:T(8,128)(2,1)S(1)} %copy-done.6), channel_id=1, source_target_pairs={{0,3},{1,0},{2,1},{3,2},{4,7},{5,4},{6,5},{7,6},{8,11},{9,8},{10,9... | collective-permute-start | bytes 786440 | tf_op jit(solution)/shard_map/ppermute | solution.py:171
  89.0 30.8 %collective-permute-start.7 = (bf16[8,64,256]{2,1,0:T(8,128)(2,1)S(1)}, bf16[8,64,256]{2,1,0:T(8,128)(2,1)S(1)}, u32[]{:S(2)}, u32[]{:S(2)}) collective-permute-start(bf16[8,64,256]{2,1,0:T(8,128)(2,1)S(1)} %copy-done.6), channel_id=1, source_target_pairs={{0,2},{1,3},{2,0},{3,1},{4,6},{5,7},{6,4},{7,5},{8,10},{9,11},{10,... | collective-permute-start | bytes 786440 | tf_op jit(solution)/shard_map/ppermute | solution.py:171
  89.3 32.2 %collective-permute-start.6 = (bf16[8,64,256]{2,1,0:T(8,128)(2,1)S(1)}, bf16[8,64,256]{2,1,0:T(8,128)(2,1)S(1)}, u32[]{:S(2)}, u32[]{:S(2)}) collective-permute-start(bf16[8,64,256]{2,1,0:T(8,128)(2,1)S(1)} %copy-done.6), channel_id=1, source_target_pairs={{0,1},{1,2},{2,3},{3,0},{4,5},{5,6},{6,7},{7,4},{8,9},{9,10},{10,1... | collective-permute-start | bytes 786440 | tf_op jit(solution)/shard_map/ppermute | solution.py:171
  92.4 24.4 %collective-permute-start.19 = (bf16[4,8,64,256]{3,2,1,0:T(8,128)(2,1)S(1)}, bf16[4,8,64,256]{3,2,1,0:T(8,128)(2,1)S(1)}, u32[]{:S(2)}, u32[]{:S(2)}) collective-permute-start(bf16[4,8,64,256]{3,2,1,0:T(8,128)(2,1)S(1)} %pad_maximum_fusion.3.refs_1_.refs_3_), channel_id=1, source_target_pairs={{0,8},{4,12},{8,0},{12,4},{16,24},{20,28},{24,16},{28,20},{1,9},{5... | collective-permute-start | bytes 3145736 | tf_op jit(solution)/shard_map/ppermute | solution.py:137
  116.8 25.5 %collective-permute-start.5 = (bf16[8,64,256]{2,1,0:T(8,128)(2,1)S(1)}, bf16[8,64,256]{2,1,0:T(8,128)(2,1)S(1)}, u32[]{:S(2)}, u32[]{:S(2)}) collective-permute-start(bf16[8,64,256]{2,1,0:T(8,128)(2,1)S(1)} %copy-done.5), channel_id=1, source_target_pairs={{0,3},{1,0},{2,1},{3,2},{4,7},{5,4},{6,5},{7,6},{8,11},{9,8},{10,9... | collective-permute-start | bytes 786440 | tf_op jit(solution)/shard_map/ppermute | solution.py:171
  119.2 23.2 %collective-permute-start.4 = (bf16[8,64,256]{2,1,0:T(8,128)(2,1)S(1)}, bf16[8,64,256]{2,1,0:T(8,128)(2,1)S(1)}, u32[]{:S(2)}, u32[]{:S(2)}) collective-permute-start(bf16[8,64,256]{2,1,0:T(8,128)(2,1)S(1)} %copy-done.5), channel_id=1, source_target_pairs={{0,2},{1,3},{2,0},{3,1},{4,6},{5,7},{6,4},{7,5},{8,10},{9,11},{10,... | collective-permute-start | bytes 786440 | tf_op jit(solution)/shard_map/ppermute | solution.py:171
  119.8 22.5 %collective-permute-start.3 = (bf16[8,64,256]{2,1,0:T(8,128)(2,1)S(1)}, bf16[8,64,256]{2,1,0:T(8,128)(2,1)S(1)}, u32[]{:S(2)}, u32[]{:S(2)}) collective-permute-start(bf16[8,64,256]{2,1,0:T(8,128)(2,1)S(1)} %copy-done.5), channel_id=1, source_target_pairs={{0,1},{1,2},{2,3},{3,0},{4,5},{5,6},{6,7},{7,4},{8,9},{9,10},{10,1... | collective-permute-start | bytes 786440 | tf_op jit(solution)/shard_map/ppermute | solution.py:171
  121.6 22.6 %collective-permute-start.20 = (bf16[4,8,64,256]{3,2,1,0:T(8,128)(2,1)S(1)}, bf16[4,8,64,256]{3,2,1,0:T(8,128)(2,1)S(1)}, u32[]{:S(2)}, u32[]{:S(2)}) collective-permute-start(bf16[4,8,64,256]{3,2,1,0:T(8,128)(2,1)S(1)} %pad_maximum_fusion.4.refs_1_), channel_id=1, source_target_pairs={{0,8},{4,12},{8,0},{12,4},{16,24},{20,28},{24,16},{28,20},{1,9},{5... | collective-permute-start | bytes 3145736 | tf_op jit(solution)/shard_map/ppermute | solution.py:137
  164.9 79.5 %collective-permute-start.21 = (bf16[10,256,1024]{2,1,0:T(8,128)(2,1)}, bf16[10,256,1024]{2,1,0:T(8,128)(2,1)}, u32[]{:S(2)}, u32[]{:S(2)}) collective-permute-start(bf16[10,256,1024]{2,1,0:T(8,128)(2,1)} %collective-permute-done.refs_0_), channel_id=1, source_target_pairs={{0,4},{4,0},{8,12},{12,8},{16,20},{20,16},{24,28},{28,24},{1,5},{5... | collective-permute-start | bytes 15728648 | tf_op jit(solution)/shard_map/ppermute | solution.py:137
  164.9 25.9 %collective-permute-start.28 = (bf16[4,8,64,256]{3,2,1,0:T(8,128)(2,1)}, bf16[4,8,64,256]{3,2,1,0:T(8,128)(2,1)}, u32[]{:S(2)}, u32[]{:S(2)}) collective-permute-start(bf16[4,8,64,256]{3,2,1,0:T(8,128)(2,1)} %pad_maximum_fusion.5.refs_1_.refs_3_), channel_id=1, source_target_pairs={{0,8},{4,12},{8,0},{12,4},{16,24},{20,28},{24,16},{28,20},{1,9},{5... | collective-permute-start | bytes 3145736 | tf_op jit(solution)/shard_map/ppermute | solution.py:137
  266.8 32.4 %collective-permute-start.25 = (bf16[8,64,256]{2,1,0:T(8,128)(2,1)S(1)}, bf16[8,64,256]{2,1,0:T(8,128)(2,1)S(1)}, u32[]{:S(2)}, u32[]{:S(2)}) collective-permute-start(bf16[8,64,256]{2,1,0:T(8,128)(2,1)S(1)} %get-tuple-element.102), channel_id=1, source_target_pairs={{0,8},{4,12},{8,0},{12,4},{16,24},{20,28},{24,16},{28,20},{1,9},{5... | collective-permute-start | bytes 786440 | tf_op jit(solution)/shard_map/ppermute | solution.py:137
  267.7 33.6 %collective-permute-start.26 = (bf16[8,64,256]{2,1,0:T(8,128)(2,1)S(1)}, bf16[8,64,256]{2,1,0:T(8,128)(2,1)S(1)}, u32[]{:S(2)}, u32[]{:S(2)}) collective-permute-start(bf16[8,64,256]{2,1,0:T(8,128)(2,1)S(1)} %get-tuple-element.103), channel_id=1, source_target_pairs={{0,16},{4,20},{8,24},{12,28},{16,0},{20,4},{24,8},{28,12},{1,17},{... | collective-permute-start | bytes 786440 | tf_op jit(solution)/shard_map/ppermute | solution.py:137
  268.2 34.1 %collective-permute-start.27 = (bf16[8,64,256]{2,1,0:T(8,128)(2,1)S(1)}, bf16[8,64,256]{2,1,0:T(8,128)(2,1)S(1)}, u32[]{:S(2)}, u32[]{:S(2)}) collective-permute-start(bf16[8,64,256]{2,1,0:T(8,128)(2,1)S(1)} %get-tuple-element.104), channel_id=1, source_target_pairs={{0,24},{4,28},{8,16},{12,20},{16,8},{20,12},{24,0},{28,4},{1,25},{... | collective-permute-start | bytes 786440 | tf_op jit(solution)/shard_map/ppermute | solution.py:137
  271.8 31.2 %collective-permute-start.22 = (bf16[8,64,256]{2,1,0:T(8,128)(2,1)S(1)}, bf16[8,64,256]{2,1,0:T(8,128)(2,1)S(1)}, u32[]{:S(2)}, u32[]{:S(2)}) collective-permute-start(bf16[8,64,256]{2,1,0:T(8,128)(2,1)S(1)} %get-tuple-element.99), channel_id=1, source_target_pairs={{0,8},{4,12},{8,0},{12,4},{16,24},{20,28},{24,16},{28,20},{1,9},{5... | collective-permute-start | bytes 786440 | tf_op jit(solution)/shard_map/ppermute | solution.py:137
  272.8 33.4 %collective-permute-start.23 = (bf16[8,64,256]{2,1,0:T(8,128)(2,1)S(1)}, bf16[8,64,256]{2,1,0:T(8,128)(2,1)S(1)}, u32[]{:S(2)}, u32[]{:S(2)}) collective-permute-start(bf16[8,64,256]{2,1,0:T(8,128)(2,1)S(1)} %get-tuple-element.100), channel_id=1, source_target_pairs={{0,16},{4,20},{8,24},{12,28},{16,0},{20,4},{24,8},{28,12},{1,17},{... | collective-permute-start | bytes 786440 | tf_op jit(solution)/shard_map/ppermute | solution.py:137
  306.2 20.1 %collective-permute-start.32 = (bf16[8,64,256]{2,1,0:T(8,128)(2,1)S(1)}, bf16[8,64,256]{2,1,0:T(8,128)(2,1)S(1)}, u32[]{:S(2)}, u32[]{:S(2)}) collective-permute-start(bf16[8,64,256]{2,1,0:T(8,128)(2,1)S(1)} %get-tuple-element.108), channel_id=1, source_target_pairs={{0,8},{4,12},{8,0},{12,4},{16,24},{20,28},{24,16},{28,20},{1,9},{5... | collective-permute-start | bytes 786440 | tf_op jit(solution)/shard_map/ppermute | solution.py:137
  (23 other events, 246.0 us)
where the time goes:
time: 336 us; the launch traced here: 335 us
  Pallas kernels  170 us (51%)
  waiting for transfers between devices  74.7 us (22%)
  starting transfers between devices  45.8 us (14%)
  local copies, waits for them, and re-layouts  34.9 us (10%)
  other arithmetic  10 us (3%)
    pallas_call x10, Pallas kernels, chain(): pl.pallas_call(kernel, out_shape=[jax.ShapeDtypeStruct((count, bands, col...  170 us
    ppermute x24, waiting for transfers between devices, send(): return lax.ppermute(value, 'val', table)  48.5 us
    ppermute x12, waiting for transfers between devices, around_z(): return [part] + [lax.ppermute(part, 'cond', to_z(q)) for q in range(1, nc)]  26.2 us
    ppermute x24, starting transfers between devices, send(): return lax.ppermute(value, 'val', table)  24.1 us
    ppermute x12, starting transfers between devices, around_z(): return [part] + [lax.ppermute(part, 'cond', to_z(q)) for q in range(1, nc)]  21.8 us
    unnamed x27, local copies, waits for them, and re-layouts  9.94 us
  transfers between devices with their start and end apart: 36, of which 14 were waited for; matrix products, arithmetic and copies ran while one was open for 9% of the time, Pallas kernels for 44%

commit v1 on v0

--- a/solution.py
+++ b/solution.py
@@ -83,13 +83,14 @@
     else:
         in_specs = [pl.BlockSpec((step_g, cols, pieces * depth), lambda i, z: (i, 0, 0))]
     flat = [unit for entry in entries for unit in entry]
-    in_specs += [pl.BlockSpec((pieces, count, rows, depth), lambda i, z: (0, 0, 0, 0)) for _ in flat]
+    in_specs += [pl.BlockSpec(
+        (pieces, count, rows, depth), lambda i, z: (0, 0, 0, 0), pipeline_mode=pl.Buffered(1)) for _ in flat]
     in_specs += [pl.BlockSpec((step_g, rows, bands), lambda i, z: (i, 0, 0)) for _ in flat]
     operands = [pc] + [t for t, _ in flat] + [pv for _, pv in flat]
     aliases = {}
     for e, acc in enumerate(accs):
         if acc is not None:
-            in_specs.append(pl.BlockSpec((count, bands, cols), fixed))
+            in_specs.append(pl.BlockSpec((count, bands, cols), fixed, pipeline_mode=pl.Buffered(1)))
             operands.append(acc)
             aliases[len(operands)] = e
     flops = 2 * len(flat) * count * total_g * rows * cols * (pieces * depth + bands)
@@ -188,7 +189,8 @@
             far.append(blocks_for(dest))
         pv_near = jnp.concatenate([mine, send(twins, to_twin)], axis=2)
         far_got = [send(f, to_x(step)) for f, step in zip(far, range(1, nx))]
-        pc_own = jnp.concatenate([pair_cond, send(after(pair_cond, block), to_twin)], axis=0)
+        pc_late = after(pair_cond, block)
+        pc_own = jnp.concatenate([pc_late, send(pc_late, to_twin)], axis=0)
         for i in range(1, CHUNKS):
             parts.append(around_z(after(block[i * n:(i + 1) * n], *far)))
 
@@ -232,11 +234,10 @@
             return token
 
         last = CHUNKS - 1
-        token = far_call([0, 1], 0, pc_y, token)
+        token = far_call([0, 1, 2, 3], 0, pc_y, token)
         for u in range(1, nx):
             (accs[last],), token = chain(
                 zed, [[(after(others[last][u - 1], token), own_pv(pv_all[u]))]], pc_own, [accs[last]])
-        token = far_call([2, 3], 0, pc_y, token)
 
         def reduced(i):
             shaped = accs[i].reshape(n, 2, nx, 2 * vb, cols)

time: 336 us -> 324 us (0.964)
  waiting for transfers between devices: 74.7 us -> 61.7 us
  starting transfers between devices: 45.8 us -> 49.4 us
    ppermute x12, waiting for transfers between devices: 26.2 us -> 15.8 us  [around_z(): return [part] + [lax.ppermute(part, 'cond', to_z(q)) for q in range(1, nc)]]
    ppermute x12, starting transfers between devices: 21.8 us -> 25.3 us  [around_z(): return [part] + [lax.ppermute(part, 'cond', to_z(q)) for q in range(1, nc)]]
    pallas_call x10 -> x9, Pallas kernels: 170 us -> 167 us  [chain(): pl.pallas_call(kernel, out_shape=[jax.ShapeDtypeStruct((count, bands, col...]
  transfers between devices with their start and end apart: 36 -> 36, of which waited for: 14 -> 14; matrix products, arithmetic and copies ran while one was open for 9% -> 9% of each run, Pallas kernels for 44% -> 45%
where the time goes in v1:
time: 324 us; the launch traced here: 323 us
  Pallas kernels  167 us (52%)
  waiting for transfers between devices  61.7 us (19%)
  starting transfers between devices  49.4 us (15%)
  local copies, waits for them, and re-layouts  34.8 us (11%)
  other arithmetic  9.89 us (3%)
    pallas_call x9, Pallas kernels, chain(): pl.pallas_call(kernel, out_shape=[jax.ShapeDtypeStruct((count, bands, col...  167 us
    ppermute x24, waiting for transfers between devices, send(): return lax.ppermute(value, 'val', table)  45.9 us
    ppermute x12, starting transfers between devices, around_z(): return [part] + [lax.ppermute(part, 'cond', to_z(q)) for q in range(1, nc)]  25.3 us
    ppermute x24, starting transfers between devices, send(): return lax.ppermute(value, 'val', table)  24 us
    ppermute x12, waiting for transfers between devices, around_z(): return [part] + [lax.ppermute(part, 'cond', to_z(q)) for q in range(1, nc)]  15.8 us
    unnamed x27, local copies, waits for them, and re-layouts  9.93 us
  transfers between devices with their start and end apart: 36, of which 14 were waited for; matrix products, arithmetic and copies ran while one was open for 9% of the time, Pallas kernels for 45%

profile of v1, /device:TPU:0, one launch (start us, length us, event | category | flops | bytes accessed | tf_op | source)
XLA Modules:
  0.0 322.9 jit_solution(16271603423577332636)
XLA Ops:
  0.0 3.0 reshape.76
  3.0 3.3 %constant_dynamic-slice_fusion.12 = (bf16[32,256,32]{2,1,0:T(8,128)(2,1)}, bf16[32,256,32]{2,1,0:T(8,128)(2,1)}) fusion(bf16[32,256,64]{2,1,0:T(8,128)(2,1)S(1)} %reshape.76, s32[]{:T(128)S(6)} %select_n.111, s32[]{:T(128)S(6)} %select_n.112), kind=kLoop, calls=%fused_computation.97 | loop fusion | bytes 2097160 | tf_op jit(solution)/shard_map/dynamic-slice
  22.4 5.4 %constant_dynamic-update-slice_fusion.1 = bf16[20,256,1024]{2,1,0:T(8,128)(2,1)} fusion(bf16[10,256,1024]{2,1,0:T(8,128)(2,1)} %param.4), kind=kLoop, calls=%fused_computation.82 | loop fusion | bytes 10485760
  31.7 5.5 %constant_dynamic-update-slice_fusion.refs_0_ = bf16[20,256,1024]{2,1,0:T(8,128)(2,1)} fusion(bf16[20,256,1024]{2,1,0:T(8,128)(2,1)} %constant_dynamic-update-slice_fusion.1, bf16[10,256,1024]{2,1,0:T(8,128)(2,1)} %collective-permute-done.2), kind=kLoop, calls=%fused_computation.81 | loop fusion | bytes 10485760 | tf_op jit(solution)/shard_map/concatenate | solution.py:193
  39.2 3.0 collective-permute-done.14
  45.1 11.5 %chain.9 = (f32[8,256,256]{2,1,0:T(8,128)}, f32[8,128]{1,0:T(8,128)}) custom-call(s32[1]{0:T(128)} %bitcast.zed_ref, bf16[20,256,1024]{2,1,0:T(8,128)(2,1)} %constant_dynamic-update-slice_fusion.refs_0_, bf16[4,8,64,256]{3,2,1,0:T(8,128)(2,1)} %copy-done.2, bf16[20,64,256]{2,1,0:T(8,128)(2,1)} %bitcast.186), custom_call_target="tpu_custom_call" | custom-call | flops 6710886400 | bytes 14680064 | tf_op jit(solution)/shard_map/chain/pallas_call | solution.py:97
  56.8 9.2 %collective-permute-start.11 = (bf16[8,64,256]{2,1,0:T(8,128)(2,1)S(1)}, bf16[8,64,256]{2,1,0:T(8,128)(2,1)S(1)}, u32[]{:S(2)}, u32[]{:S(2)}) collective-permute-start(bf16[8,64,256]{2,1,0:T(8,128)(2,1)S(1)} %copy-done.7), channel_id=1, source_target_pairs={{0,3},{1,0},{2,1},{3,2},{4,7},{5,4},{6,5},{7,6},{8,11},{9,8},{10,9... | collective-permute-start | bytes 786440 | tf_op jit(solution)/shard_map/ppermute | solution.py:172
  66.0 6.7 %collective-permute-done.11 = bf16[8,64,256]{2,1,0:T(8,128)(2,1)S(1)} collective-permute-done((bf16[8,64,256]{2,1,0:T(8,128)(2,1)S(1)}, bf16[8,64,256]{2,1,0:T(8,128)(2,1)S(1)}, u32[]{:S(2)}, u32[]{:S(2)}) %collective-permute-start.11) | collective-permute-done | bytes 262176 | tf_op jit(solution)/shard_map/ppermute | solution.py:172
  72.7 6.0 %collective-permute-done.9 = bf16[8,64,256]{2,1,0:T(8,128)(2,1)S(1)} collective-permute-done((bf16[8,64,256]{2,1,0:T(8,128)(2,1)S(1)}, bf16[8,64,256]{2,1,0:T(8,128)(2,1)S(1)}, u32[]{:S(2)}, u32[]{:S(2)}) %collective-permute-start.9) | collective-permute-done | bytes 262176 | tf_op jit(solution)/shard_map/ppermute | solution.py:172
  80.5 3.1 collective-permute-start.8
  85.5 19.8 %chain.10 = (f32[8,256,256]{2,1,0:T(8,128)}, f32[8,256,256]{2,1,0:T(8,128)}, f32[8,128]{1,0:T(8,128)}) custom-call(s32[1]{0:T(128)} %bitcast.zed_ref, bf16[20,256,1024]{2,1,0:T(8,128)(2,1)} %constant_dynamic-update-slice_fusion.refs_0_, bf16[4,8,64,256]{3,2,1,0:T(8,128)(2,1)} %copy-done.3, ...), custom_call_target="tpu_custom_call", output_to_operand_aliasing={{1}: (6, {})} | custom-call | flops 13421772800 | bytes 18874368 | tf_op jit(solution)/shard_map/chain/pallas_call | solution.py:97
  105.3 3.0 collective-permute-done.19.refs_2_.refs_4_
  109.2 2.9 collective-permute-start.5
  113.3 19.7 %chain.11 = (f32[8,256,256]{2,1,0:T(8,128)}, f32[8,256,256]{2,1,0:T(8,128)}, f32[8,128]{1,0:T(8,128)}) custom-call(s32[1]{0:T(128)} %bitcast.zed_ref, bf16[20,256,1024]{2,1,0:T(8,128)(2,1)} %constant_dynamic-update-slice_fusion.refs_0_, bf16[4,8,64,256]{3,2,1,0:T(8,128)(2,1)} %copy-done.4, ...), custom_call_target="tpu_custom_call", output_to_operand_aliasing={{1}: (6, {})} | custom-call | flops 13421772800 | bytes 18874368 | tf_op jit(solution)/shard_map/chain/pallas_call | solution.py:97
  135.7 19.7 %chain.12 = (f32[8,256,256]{2,1,0:T(8,128)}, f32[8,256,256]{2,1,0:T(8,128)}, f32[8,128]{1,0:T(8,128)}) custom-call(s32[1]{0:T(128)} %bitcast.zed_ref, bf16[20,256,1024]{2,1,0:T(8,128)(2,1)} %constant_dynamic-update-slice_fusion.refs_0_, bf16[4,8,64,256]{3,2,1,0:T(8,128)(2,1)} %pad_maximum_fusion.5.refs_1_.refs_7_, ...), custom_call_target="tpu_custom_call", output_to_operand_aliasing={{1}: (6, {})} | custom-call | flops 13421772800 | bytes 18874368 | tf_op jit(solution)/shard_map/chain/pallas_call | solution.py:97
  158.3 23.1 %collective-permute-done.22.refs_8_.refs_1_.refs_2_ = bf16[4,8,64,256]{3,2,1,0:T(8,128)(2,1)} collective-permute-done((bf16[4,8,64,256]{3,2,1,0:T(8,128)(2,1)}, bf16[4,8,64,256]{3,2,1,0:T(8,128)(2,1)}, u32[]{:S(2)}, u32[]{:S(2)}) %collective-permute-start.22) | collective-permute-done | bytes 1048608 | tf_op jit(solution)/shard_map/ppermute | solution.py:138
  181.4 38.5 %chain.13 = (f32[8,256,256]{2,1,0:T(8,128)}, f32[8,256,256]{2,1,0:T(8,128)}, f32[8,256,256]{2,1,0:T(8,128)}, f32[8,256,256]{2,1,0:T(8,128)}, f32[8,128]{1,0:T(8,128)}) custom-call(s32[1]{0:T(128)} %bitcast.zed_ref, bf16[10,256,1024]{2,1,0:T(8,128)(2,1)} %collective-permute-done.refs_0_, ...), custom_call_target="tpu_custom_call", output_to_operand_aliasing={{0}: (18, {}), {1}: (19, {}), {2}: (20, {}), {3}: (21, {})} | custom-call | flops 26843545600 | bytes 22020096 | tf_op jit(solution)/shard_map/chain/pallas_call | solution.py:97
  219.9 12.1 %chain.16 = (f32[8,256,256]{2,1,0:T(8,128)}, f32[8,128]{1,0:T(8,128)}) custom-call(s32[1]{0:T(128)} %bitcast.zed_ref, bf16[20,256,1024]{2,1,0:T(8,128)(2,1)} %constant_dynamic-update-slice_fusion.refs_0_, bf16[4,8,64,256]{3,2,1,0:T(8,128)(2,1)} %collective-permute-done.22.refs_8_.refs_1_.refs_2_, ...), custom_call_target="tpu_custom_call", output_to_operand_aliasing={{0}: (4, {})} | custom-call | flops 6710886400 | bytes 14680064 | tf_op jit(solution)/shard_map/chain/pallas_call | solution.py:97
  232.0 20.9 %chain.14 = (f32[8,256,256]{2,1,0:T(8,128)}, f32[8,256,256]{2,1,0:T(8,128)}, f32[8,128]{1,0:T(8,128)}) custom-call(s32[1]{0:T(128)} %bitcast.zed_ref, bf16[10,256,1024]{2,1,0:T(8,128)(2,1)} %collective-permute-done.21.refs_0_, bf16[4,8,64,256]{3,2,1,0:T(8,128)(2,1)} %copy-done.2, ...), custom_call_target="tpu_custom_call", output_to_operand_aliasing={{0}: (10, {}), {1}: (11, {})} | custom-call | flops 13421772800 | bytes 13631488 | tf_op jit(solution)/shard_map/chain/pallas_call | solution.py:97
  260.9 12.1 %chain.15 = (f32[8,256,256]{2,1,0:T(8,128)}, f32[8,128]{1,0:T(8,128)}) custom-call(s32[1]{0:T(128)} %bitcast.zed_ref, bf16[10,256,1024]{2,1,0:T(8,128)(2,1)} %collective-permute-done.21.refs_0_, bf16[4,8,64,256]{3,2,1,0:T(8,128)(2,1)} %copy-done.4, bf16[4,8,64,256]{3,2,1,0:T(8,128)(2,1)} %copy-done.10, ...), custom_call_target="tpu_custom_call", output_to_operand_aliasing={{0}: (6, {})} | custom-call | flops 6710886400 | bytes 9437184 | tf_op jit(solution)/shard_map/chain/pallas_call | solution.py:97
  273.1 12.3 %chain.17 = (f32[8,256,256]{2,1,0:T(8,128)}, f32[8,128]{1,0:T(8,128)}) custom-call(s32[1]{0:T(128)} %bitcast.zed_ref, bf16[10,256,1024]{2,1,0:T(8,128)(2,1)} %collective-permute-done.21.refs_0_, bf16[4,8,64,256]{3,2,1,0:T(8,128)(2,1)} %pad_maximum_fusion.5.refs_1_.refs_7_, ...), custom_call_target="tpu_custom_call", output_to_operand_aliasing={{0}: (6, {})} | custom-call | flops 6710886400 | bytes 9437184 | tf_op jit(solution)/shard_map/chain/pallas_call | solution.py:97
  297.2 4.2 %collective-permute-done.29 = bf16[8,64,256]{2,1,0:T(8,128)(2,1)S(1)} collective-permute-done((bf16[8,64,256]{2,1,0:T(8,128)(2,1)S(1)}, bf16[8,64,256]{2,1,0:T(8,128)(2,1)S(1)}, u32[]{:S(2)}, u32[]{:S(2)}) %collective-permute-start.29) | collective-permute-done | bytes 262176 | tf_op jit(solution)/shard_map/ppermute | solution.py:138
  307.1 5.5 %collective-permute-done.32 = bf16[8,64,256]{2,1,0:T(8,128)(2,1)S(1)} collective-permute-done((bf16[8,64,256]{2,1,0:T(8,128)(2,1)S(1)}, bf16[8,64,256]{2,1,0:T(8,128)(2,1)S(1)}, u32[]{:S(2)}, u32[]{:S(2)}) %collective-permute-start.32) | collective-permute-done | bytes 262176 | tf_op jit(solution)/shard_map/ppermute | solution.py:138
  312.6 2.9 collective-permute-done.33
  (124 shorter events, 69.0 us)
Async XLA Ops:
  10.8 19.3 %collective-permute-start.2 = (bf16[10,256,1024]{2,1,0:T(8,128)(2,1)}, bf16[10,256,1024]{2,1,0:T(8,128)(2,1)}, u32[]{:S(2)}, u32[]{:S(2)}) collective-permute-start(bf16[10,256,1024]{2,1,0:T(8,128)(2,1)} %param.4), channel_id=1, source_target_pairs={{0,4},{4,0},{8,12},{12,8},{16,20},{20,16},{24,28},{28,24},{1,5},{5... | collective-permute-start | bytes 15728648 | tf_op jit(solution)/shard_map/ppermute | solution.py:138
  11.2 144.2 %collective-permute-start = (bf16[10,256,1024]{2,1,0:T(8,128)(2,1)}, bf16[10,256,1024]{2,1,0:T(8,128)(2,1)}, u32[]{:S(2)}, u32[]{:S(2)}) collective-permute-start(bf16[10,256,1024]{2,1,0:T(8,128)(2,1)} %param.4), channel_id=1, source_target_pairs={{0,16},{4,20},{8,24},{12,28},{16,0},{20,4},{24,8},{28,12},{1,17},{... | collective-permute-start | bytes 15728648 | tf_op jit(solution)/shard_map/ppermute | solution.py:138
  15.9 21.2 %collective-permute-start.12 = (bf16[8,64,256]{2,1,0:T(8,128)(2,1)}, bf16[8,64,256]{2,1,0:T(8,128)(2,1)}, u32[]{:S(2)}, u32[]{:S(2)}) collective-permute-start(bf16[8,64,256]{2,1,0:T(8,128)(2,1)} %get-tuple-element.57), channel_id=1, source_target_pairs={{0,1},{1,2},{2,3},{3,0},{4,5},{5,6},{6,7},{7,4},{8,9},{9,10},{10,1... | collective-permute-start | bytes 786440 | tf_op jit(solution)/shard_map/ppermute | solution.py:172
  17.5 21.7 %collective-permute-start.13 = (bf16[8,64,256]{2,1,0:T(8,128)(2,1)}, bf16[8,64,256]{2,1,0:T(8,128)(2,1)}, u32[]{:S(2)}, u32[]{:S(2)}) collective-permute-start(bf16[8,64,256]{2,1,0:T(8,128)(2,1)} %get-tuple-element.57), channel_id=1, source_target_pairs={{0,2},{1,3},{2,0},{3,1},{4,6},{5,7},{6,4},{7,5},{8,10},{9,11},{10,... | collective-permute-start | bytes 786440 | tf_op jit(solution)/shard_map/ppermute | solution.py:172
  30.2 26.4 %collective-permute-start.17 = (bf16[4,10,32,256]{3,2,1,0:T(8,128)(2,1)S(1)}, bf16[4,10,32,256]{3,2,1,0:T(8,128)(2,1)S(1)}, u32[]{:S(2)}, u32[]{:S(2)}) collective-permute-start(bf16[4,10,32,256]{3,2,1,0:T(8,128)(2,1)S(1)} %pad_maximum_fusion.7), channel_id=1, source_target_pairs={{0,8},{4,12},{8,0},{12,4},{16,24},{20,28},{24,16},{28,20},{1,9},{5... | collective-permute-start | bytes 1966088 | tf_op jit(solution)/shard_map/ppermute | solution.py:138
  37.1 28.8 %collective-permute-start.10 = (bf16[8,64,256]{2,1,0:T(8,128)(2,1)S(1)}, bf16[8,64,256]{2,1,0:T(8,128)(2,1)S(1)}, u32[]{:S(2)}, u32[]{:S(2)}) collective-permute-start(bf16[8,64,256]{2,1,0:T(8,128)(2,1)S(1)} %copy-done.7), channel_id=1, source_target_pairs={{0,2},{1,3},{2,0},{3,1},{4,6},{5,7},{6,4},{7,5},{8,10},{9,11},{10,... | collective-permute-start | bytes 786440 | tf_op jit(solution)/shard_map/ppermute | solution.py:172
  43.5 41.1 %collective-permute-start.16 = (bf16[4,8,64,256]{3,2,1,0:T(8,128)(2,1)S(1)}, bf16[4,8,64,256]{3,2,1,0:T(8,128)(2,1)}, u32[]{:S(2)}, u32[]{:S(2)}) collective-permute-start(bf16[4,8,64,256]{3,2,1,0:T(8,128)(2,1)S(1)} %pad_maximum_fusion.2.refs_1_), channel_id=1, source_target_pairs={{0,8},{4,12},{8,0},{12,4},{16,24},{20,28},{24,16},{28,20},{1,9},{5... | collective-permute-start | bytes 3145736 | tf_op jit(solution)/shard_map/ppermute | solution.py:138
  56.7 23.8 %collective-permute-start.18 = (bf16[4,10,32,256]{3,2,1,0:T(8,128)(2,1)S(1)}, bf16[4,10,32,256]{3,2,1,0:T(8,128)(2,1)S(1)}, u32[]{:S(2)}, u32[]{:S(2)}) collective-permute-start(bf16[4,10,32,256]{3,2,1,0:T(8,128)(2,1)S(1)} %pad_maximum_fusion.9), channel_id=1, source_target_pairs={{0,4},{4,0},{8,12},{12,8},{16,20},{20,16},{24,28},{28,24},{1,5},{5... | collective-permute-start | bytes 1966088 | tf_op jit(solution)/shard_map/ppermute | solution.py:138
  72.7 35.6 %collective-permute-start.6 = (bf16[8,64,256]{2,1,0:T(8,128)(2,1)S(1)}, bf16[8,64,256]{2,1,0:T(8,128)(2,1)S(1)}, u32[]{:S(2)}, u32[]{:S(2)}) collective-permute-start(bf16[8,64,256]{2,1,0:T(8,128)(2,1)S(1)} %copy-done.6), channel_id=1, source_target_pairs={{0,1},{1,2},{2,3},{3,0},{4,5},{5,6},{6,7},{7,4},{8,9},{9,10},{10,1... | collective-permute-start | bytes 786440 | tf_op jit(solution)/shard_map/ppermute | solution.py:172
  78.7 30.5 %collective-permute-start.7 = (bf16[8,64,256]{2,1,0:T(8,128)(2,1)S(1)}, bf16[8,64,256]{2,1,0:T(8,128)(2,1)S(1)}, u32[]{:S(2)}, u32[]{:S(2)}) collective-permute-start(bf16[8,64,256]{2,1,0:T(8,128)(2,1)S(1)} %copy-done.6), channel_id=1, source_target_pairs={{0,2},{1,3},{2,0},{3,1},{4,6},{5,7},{6,4},{7,5},{8,10},{9,11},{10,... | collective-permute-start | bytes 786440 | tf_op jit(solution)/shard_map/ppermute | solution.py:172
  80.5 31.6 %collective-permute-start.8 = (bf16[8,64,256]{2,1,0:T(8,128)(2,1)S(1)}, bf16[8,64,256]{2,1,0:T(8,128)(2,1)S(1)}, u32[]{:S(2)}, u32[]{:S(2)}) collective-permute-start(bf16[8,64,256]{2,1,0:T(8,128)(2,1)S(1)} %copy-done.6), channel_id=1, source_target_pairs={{0,3},{1,0},{2,1},{3,2},{4,7},{5,4},{6,5},{7,6},{8,11},{9,8},{10,9... | collective-permute-start | bytes 786440 | tf_op jit(solution)/shard_map/ppermute | solution.py:172
  84.6 23.7 %collective-permute-start.19 = (bf16[4,8,64,256]{3,2,1,0:T(8,128)(2,1)S(1)}, bf16[4,8,64,256]{3,2,1,0:T(8,128)(2,1)S(1)}, u32[]{:S(2)}, u32[]{:S(2)}) collective-permute-start(bf16[4,8,64,256]{3,2,1,0:T(8,128)(2,1)S(1)} %pad_maximum_fusion.3.refs_1_.refs_3_), channel_id=1, source_target_pairs={{0,8},{4,12},{8,0},{12,4},{16,24},{20,28},{24,16},{28,20},{1,9},{5... | collective-permute-start | bytes 3145736 | tf_op jit(solution)/shard_map/ppermute | solution.py:138
  108.2 24.7 %collective-permute-start.3 = (bf16[8,64,256]{2,1,0:T(8,128)(2,1)S(1)}, bf16[8,64,256]{2,1,0:T(8,128)(2,1)S(1)}, u32[]{:S(2)}, u32[]{:S(2)}) collective-permute-start(bf16[8,64,256]{2,1,0:T(8,128)(2,1)S(1)} %copy-done.5), channel_id=1, source_target_pairs={{0,1},{1,2},{2,3},{3,0},{4,5},{5,6},{6,7},{7,4},{8,9},{9,10},{10,1... | collective-permute-start | bytes 786440 | tf_op jit(solution)/shard_map/ppermute | solution.py:172
  108.3 24.7 %collective-permute-start.4 = (bf16[8,64,256]{2,1,0:T(8,128)(2,1)S(1)}, bf16[8,64,256]{2,1,0:T(8,128)(2,1)S(1)}, u32[]{:S(2)}, u32[]{:S(2)}) collective-permute-start(bf16[8,64,256]{2,1,0:T(8,128)(2,1)S(1)} %copy-done.5), channel_id=1, source_target_pairs={{0,2},{1,3},{2,0},{3,1},{4,6},{5,7},{6,4},{7,5},{8,10},{9,11},{10,... | collective-permute-start | bytes 786440 | tf_op jit(solution)/shard_map/ppermute | solution.py:172
  109.2 23.8 %collective-permute-start.5 = (bf16[8,64,256]{2,1,0:T(8,128)(2,1)S(1)}, bf16[8,64,256]{2,1,0:T(8,128)(2,1)S(1)}, u32[]{:S(2)}, u32[]{:S(2)}) collective-permute-start(bf16[8,64,256]{2,1,0:T(8,128)(2,1)S(1)} %copy-done.5), channel_id=1, source_target_pairs={{0,3},{1,0},{2,1},{3,2},{4,7},{5,4},{6,5},{7,6},{8,11},{9,8},{10,9... | collective-permute-start | bytes 786440 | tf_op jit(solution)/shard_map/ppermute | solution.py:172
  112.3 22.4 %collective-permute-start.20 = (bf16[4,8,64,256]{3,2,1,0:T(8,128)(2,1)S(1)}, bf16[4,8,64,256]{3,2,1,0:T(8,128)(2,1)S(1)}, u32[]{:S(2)}, u32[]{:S(2)}) collective-permute-start(bf16[4,8,64,256]{3,2,1,0:T(8,128)(2,1)S(1)} %pad_maximum_fusion.4.refs_1_.refs_5_), channel_id=1, source_target_pairs={{0,8},{4,12},{8,0},{12,4},{16,24},{20,28},{24,16},{28,20},{1,9},{5... | collective-permute-start | bytes 3145736 | tf_op jit(solution)/shard_map/ppermute | solution.py:138
  155.4 76.6 %collective-permute-start.21 = (bf16[10,256,1024]{2,1,0:T(8,128)(2,1)}, bf16[10,256,1024]{2,1,0:T(8,128)(2,1)}, u32[]{:S(2)}, u32[]{:S(2)}) collective-permute-start(bf16[10,256,1024]{2,1,0:T(8,128)(2,1)} %collective-permute-done.refs_0_), channel_id=1, source_target_pairs={{0,4},{4,0},{8,12},{12,8},{16,20},{20,16},{24,28},{28,24},{1,5},{5... | collective-permute-start | bytes 15728648 | tf_op jit(solution)/shard_map/ppermute | solution.py:138
  155.5 25.9 %collective-permute-start.22 = (bf16[4,8,64,256]{3,2,1,0:T(8,128)(2,1)}, bf16[4,8,64,256]{3,2,1,0:T(8,128)(2,1)}, u32[]{:S(2)}, u32[]{:S(2)}) collective-permute-start(bf16[4,8,64,256]{3,2,1,0:T(8,128)(2,1)} %pad_maximum_fusion.5.refs_1_.refs_7_), channel_id=1, source_target_pairs={{0,8},{4,12},{8,0},{12,4},{16,24},{20,28},{24,16},{28,20},{1,9},{5... | collective-permute-start | bytes 3145736 | tf_op jit(solution)/shard_map/ppermute | solution.py:138
  254.4 31.1 %collective-permute-start.23 = (bf16[8,64,256]{2,1,0:T(8,128)(2,1)S(1)}, bf16[8,64,256]{2,1,0:T(8,128)(2,1)S(1)}, u32[]{:S(2)}, u32[]{:S(2)}) collective-permute-start(bf16[8,64,256]{2,1,0:T(8,128)(2,1)S(1)} %get-tuple-element.99), channel_id=1, source_target_pairs={{0,8},{4,12},{8,0},{12,4},{16,24},{20,28},{24,16},{28,20},{1,9},{5... | collective-permute-start | bytes 786440 | tf_op jit(solution)/shard_map/ppermute | solution.py:138
  255.4 32.3 %collective-permute-start.24 = (bf16[8,64,256]{2,1,0:T(8,128)(2,1)S(1)}, bf16[8,64,256]{2,1,0:T(8,128)(2,1)S(1)}, u32[]{:S(2)}, u32[]{:S(2)}) collective-permute-start(bf16[8,64,256]{2,1,0:T(8,128)(2,1)S(1)} %get-tuple-element.100), channel_id=1, source_target_pairs={{0,16},{4,20},{8,24},{12,28},{16,0},{20,4},{24,8},{28,12},{1,17},{... | collective-permute-start | bytes 786440 | tf_op jit(solution)/shard_map/ppermute | solution.py:138
  255.9 34.1 %collective-permute-start.25 = (bf16[8,64,256]{2,1,0:T(8,128)(2,1)S(1)}, bf16[8,64,256]{2,1,0:T(8,128)(2,1)S(1)}, u32[]{:S(2)}, u32[]{:S(2)}) collective-permute-start(bf16[8,64,256]{2,1,0:T(8,128)(2,1)S(1)} %get-tuple-element.101), channel_id=1, source_target_pairs={{0,24},{4,28},{8,16},{12,20},{16,8},{20,12},{24,0},{28,4},{1,25},{... | collective-permute-start | bytes 786440 | tf_op jit(solution)/shard_map/ppermute | solution.py:138
  259.5 31.2 %collective-permute-start.26 = (bf16[8,64,256]{2,1,0:T(8,128)(2,1)S(1)}, bf16[8,64,256]{2,1,0:T(8,128)(2,1)S(1)}, u32[]{:S(2)}, u32[]{:S(2)}) collective-permute-start(bf16[8,64,256]{2,1,0:T(8,128)(2,1)S(1)} %get-tuple-element.102), channel_id=1, source_target_pairs={{0,8},{4,12},{8,0},{12,4},{16,24},{20,28},{24,16},{28,20},{1,9},{5... | collective-permute-start | bytes 786440 | tf_op jit(solution)/shard_map/ppermute | solution.py:138
  260.4 33.5 %collective-permute-start.27 = (bf16[8,64,256]{2,1,0:T(8,128)(2,1)S(1)}, bf16[8,64,256]{2,1,0:T(8,128)(2,1)S(1)}, u32[]{:S(2)}, u32[]{:S(2)}) collective-permute-start(bf16[8,64,256]{2,1,0:T(8,128)(2,1)S(1)} %get-tuple-element.103), channel_id=1, source_target_pairs={{0,16},{4,20},{8,24},{12,28},{16,0},{20,4},{24,8},{28,12},{1,17},{... | collective-permute-start | bytes 786440 | tf_op jit(solution)/shard_map/ppermute | solution.py:138
  295.7 19.8 %collective-permute-start.33 = (bf16[8,64,256]{2,1,0:T(8,128)(2,1)S(1)}, bf16[8,64,256]{2,1,0:T(8,128)(2,1)S(1)}, u32[]{:S(2)}, u32[]{:S(2)}) collective-permute-start(bf16[8,64,256]{2,1,0:T(8,128)(2,1)S(1)} %get-tuple-element.110), channel_id=1, source_target_pairs={{0,16},{4,20},{8,24},{12,28},{16,0},{20,4},{24,8},{28,12},{1,17},{... | collective-permute-start | bytes 786440 | tf_op jit(solution)/shard_map/ppermute | solution.py:138
  (23 other events, 225.6 us)
